TPU v7x, 32 devices: a whole 2x2x4 slice. The times are simulated.
32 devices in a mesh: ta: 16 (over z, x, core), aa: 2 (over y).
Axes of the slice: x: 2, y: 2, z: 4, core: 2. Of those that a mesh axis runs over, the one named last changes fastest.
Arguments:
- voltages: bfloat16 [256, 393216], P('aa', 'ta'), may hold values from -6 to 6
- pfb_window: float32 [4, 8192], replicated, may hold values from -3 to 3
Outputs:
- visibilities: float32 [2048, 256, 512], P('ta', 'aa')
All inputs are finite; a program needn't handle non-finite values.
Results may differ from a plain program's by a relative error of at most 0.0026.
Values may be sent and summed in bfloat16 or wider, within the bound.
A program may use at most 192 MiB of HBM per device.

v0:
```python
import functools
import math

import jax
import jax.numpy as jnp
import numpy as np
from jax import lax
from jax.experimental import pallas as pl
from jax.experimental.pallas import tpu as pltpu
from jax.sharding import PartitionSpec as P

NFFT = 8192
CH = 2048
TAPS = 4
CH_OFF = 1024
RADIX = 32
INNER = NFFT // RADIX
BINS = CH // RADIX
HALF = RADIX // 2
LANES = 128
SIG_BLOCK = 16
LEFT = TAPS - 2
MESH = pl.DeviceIdType.MESH


def split_bf16(x):
    hi = jnp.asarray(x, jnp.bfloat16)
    return hi, (x - hi.astype(jnp.float32)).astype(jnp.bfloat16)


def stage_two_matrix():
    n2 = np.arange(INNER)[None, :]
    m = np.arange(BINS)[:, None] + CH_OFF // RADIX
    angle = 2.0 * np.pi * ((n2 * m) % INNER) / INNER
    mirror = 2.0 * np.pi * ((n2 * (m + 1)) % INNER) / INNER
    rows = [
        np.concatenate([np.cos(angle), np.sin(angle)], axis=1),
        np.concatenate([-np.sin(angle), np.cos(angle)], axis=1),
        np.concatenate([np.cos(mirror), -np.sin(mirror)], axis=1),
        np.concatenate([-np.sin(mirror), -np.cos(mirror)], axis=1),
    ]
    full = np.concatenate(rows, axis=0) / math.sqrt(NFFT)
    hi = full.astype(jnp.bfloat16)
    lo = (full - hi.astype(np.float64)).astype(jnp.bfloat16)
    return hi, lo


def twist_table():
    k = np.arange(HALF + 1)[:, None]
    n2 = np.arange(INNER)[None, :]
    angle = 2.0 * np.pi * (k * n2) / NFFT
    return np.stack([np.cos(angle), -np.sin(angle)]).astype(np.float32)


def rfft_list(x):
    n = len(x)
    if n == 2:
        return [(x[0] + x[1], None), (x[0] - x[1], None)]
    even, odd = rfft_list(x[0::2]), rfft_list(x[1::2])
    out = [None] * (n // 2 + 1)
    for k in range(n // 4 + 1):
        er, ei = even[k]
        our, oui = odd[k]
        if k == 0:
            out[0] = (er + our, None)
            out[n // 2] = (er - our, None)
        elif k == n // 4:
            out[k] = (er, -our)
        else:
            c = math.cos(2 * math.pi * k / n)
            s = math.sin(2 * math.pi * k / n)
            if 8 * k == n:
                tr, ti = (our + oui) * c, (oui - our) * c
            else:
                tr, ti = our * c + oui * s, oui * c - our * s
            out[k] = (er + tr, ei + ti)
            out[n // 2 - k] = (er - tr, ti - ei)
    return out


def channel_frame(signals, first, here_at, volts, win, twist, mat_hi, mat_lo, parts_s, spec_s, out):
    def block(step, carry):
        rows = pl.ds(pl.multiple_of(step * SIG_BLOCK, SIG_BLOCK), SIG_BLOCK)
        low_rows = pl.ds(pl.multiple_of(signals + step * SIG_BLOCK, SIG_BLOCK), SIG_BLOCK)
        for part in range(INNER // LANES):
            filtered = []
            for n1 in range(RADIX):
                cols = pl.ds(n1 * INNER + part * LANES, LANES)
                total = win[0:1, cols] * volts[first, rows, cols].astype(jnp.float32)
                for t in range(1, TAPS):
                    total = total + win[t : t + 1, cols] * volts[first + t, rows, cols].astype(jnp.float32)
                filtered.append(total)
            here = pl.ds(part * LANES, LANES)
            there = pl.ds(INNER + part * LANES, LANES)
            for k, (ar, ai) in enumerate(rfft_list(filtered)):
                if k == 0:
                    br, bi = ar, jnp.zeros_like(ar)
                else:
                    tr, ti = twist[0, k : k + 1, here], twist[1, k : k + 1, here]
                    if ai is None:
                        br, bi = ar * tr, ar * ti
                    else:
                        br, bi = ar * tr - ai * ti, ar * ti + ai * tr
                for value, cols in ((br, here), (bi, there)):
                    hi, lo = split_bf16(value)
                    parts_s[k, rows, cols] = hi
                    parts_s[k, low_rows, cols] = lo
        return carry

    lax.fori_loop(0, signals // SIG_BLOCK, block, 0)
    dims = (((1,), (1,)), ((), ()))

    def dot(a, b):
        return lax.dot_general(a, b, dims, preferred_element_type=jnp.float32)

    def put(value, k):
        spec_s[pl.ds(2 * k, BINS, stride=2 * RADIX), :] = value[:BINS]
        spec_s[pl.ds(2 * k + 1, BINS, stride=2 * RADIX), :] = value[BINS:]

    for k in range(HALF + 1):
        size = 2 * BINS if k in (0, HALF) else 4 * BINS
        a_hi, a_lo = mat_hi[:size, :], mat_lo[:size, :]
        both = dot(a_hi, parts_s[k])
        small = dot(a_lo, parts_s[k, :signals])
        res = both[:, :signals] + (both[:, signals:] + small)
        put(res[: 2 * BINS], k)
        if size > 2 * BINS:
            put(res[2 * BINS :], RADIX - k)

    flat = out.at[here_at].reshape(2 * CH, signals)

    def cast(i, carry):
        at = pl.ds(pl.multiple_of(i * 128, 128), 128)
        flat[at, :] = spec_s[at, :].astype(jnp.bfloat16)
        return carry

    lax.fori_loop(0, 2 * CH // 128, cast, 0)


def exchange_kernel(signals, frames, peers, vol, win, twist, mat_hi, mat_lo, grid_out,
                    volts, wmask, parts_s, spec_s, spec,
                    load_sem, halo_send, halo_recv, own_sem, send_sem, recv_sem, over_send, over_recv):
    ta, aa = lax.axis_index("ta"), lax.axis_index("aa")
    core = ta % 2
    last = peers - 1
    mine = CH // peers
    right, left = (ta + 1) % peers, (ta + last) % peers

    load = pltpu.make_async_copy
    loads = [
        load(vol.at[:, pl.ds(f * NFFT, NFFT)], volts.at[LEFT + f], load_sem.at[f])
        for f in range(frames)
    ]
    for copy in loads:
        copy.start()

    barrier = pltpu.get_barrier_semaphore()

    def greet(i, carry):
        pl.semaphore_signal(barrier, 1, device_id=((ta + i) % peers, aa), device_id_type=MESH)
        return carry

    lax.fori_loop(1, peers, greet, 0)
    pl.semaphore_signal(barrier, 1, device_id=(ta, 1 - aa), device_id_type=MESH)
    pl.semaphore_wait(barrier, peers)

    def to_right(slot):
        return pltpu.make_async_remote_copy(
            vol.at[:, pl.ds((frames - LEFT + slot) * NFFT, NFFT)], volts.at[slot],
            halo_send.at[slot], halo_recv.at[slot],
            device_id=(right, aa), device_id_type=MESH)

    to_left = pltpu.make_async_remote_copy(
        vol.at[:, pl.ds(0, NFFT)], volts.at[LEFT + frames],
        halo_send.at[LEFT], halo_recv.at[LEFT],
        device_id=(left, aa), device_id_type=MESH)

    @pl.when(ta < last)
    def _():
        for slot in reversed(range(LEFT)):
            to_right(slot).start()

    to_left.start()

    @pl.when(ta == 0)
    def _():
        def clear(i, carry):
            rows = pl.ds(pl.multiple_of(i * SIG_BLOCK, SIG_BLOCK), SIG_BLOCK)
            for slot in range(LEFT):
                volts[slot, rows, :] = jnp.zeros((SIG_BLOCK, NFFT), jnp.bfloat16)
            return carry

        lax.fori_loop(0, signals // SIG_BLOCK, clear, 0)

    for copy in loads:
        copy.wait()

    def send(step, frame, i):
        to = (ta + i) % peers
        return pltpu.make_async_remote_copy(
            spec.at[step, pl.ds(to * mine, mine)], grid_out.at[aa, :, frame * peers + ta],
            send_sem.at[frame, i], recv_sem.at[frame, i],
            device_id=(to, aa), device_id_type=MESH)

    def keep(step, frame):
        return load(spec.at[step, pl.ds(ta * mine, mine)], grid_out.at[aa, :, frame * peers + ta],
                    own_sem.at[frame])

    def over_own(step, frame):
        return pltpu.make_async_remote_copy(
            spec.at[step, pl.ds(ta * mine, mine)], grid_out.at[aa, :, frame * peers + ta],
            over_send.at[frame, 0], over_recv.at[frame, 0],
            device_id=(ta, 1 - aa), device_id_type=MESH)

    def arrival(frame, i):
        source = (ta + peers - i) % peers
        place = grid_out.at[aa, :, frame * peers + source]
        return pltpu.make_async_remote_copy(
            place, place, send_sem.at[frame, i], recv_sem.at[frame, i],
            device_id=(source, aa), device_id_type=MESH)

    def over(side, frame, i):
        source = (ta + peers - i) % peers
        place = grid_out.at[side, :, frame * peers + source]
        return pltpu.make_async_remote_copy(
            place, place, over_send.at[frame, i], over_recv.at[frame, i],
            device_id=(ta, 1 - aa), device_id_type=MESH)

    def outward(n):
        return peers // 2 + jnp.where(n % 2 == 0, n // 2, -((n + 1) // 2))

    def frame_at(step):
        return jnp.where(core == 0, frames - 1 - step, step)

    def one_step(step, carry):
        frame = frame_at(step)

        @pl.when((step == 0) & (core == 0) | (step == frames - 1) & (core == 1))
        def _():
            to_left.wait_recv()

        for slot in range(LEFT):
            when = jnp.where(core == 0, frames - 1 - slot, 0)

            @pl.when((step == when) & (ta > 0))
            def _():
                to_right(slot).wait_recv()

        first_tap = (ta == last) & (frame == frames - 1)
        keep_old = jnp.where(first_tap, 0.0, 1.0).astype(jnp.float32)
        wmask[0 : TAPS - 1, :] = win[0 : TAPS - 1, :] * keep_old
        wmask[TAPS - 1 : TAPS, :] = win[TAPS - 1 : TAPS, :]
        channel_frame(signals, frame, step, volts, wmask, twist, mat_hi, mat_lo, parts_s, spec_s, spec)

        def each(n, c):
            send(step, frame, outward(n)).start()
            return c

        lax.fori_loop(0, peers - 1, each, 0)
        over_own(step, frame).start()
        keep(step, frame).start()
        return carry

    lax.fori_loop(0, frames, one_step, 0)

    def forward(at, carry):
        step, n = at // (peers - 1), at % (peers - 1)
        i = outward(peers - 2 - n)
        source = (ta + peers - i) % peers
        frame = jnp.where(source % 2 == 0, frames - 1 - step, step)
        arrival(frame, i).wait_recv()
        over(aa, frame, i).start()
        return carry

    lax.fori_loop(0, frames * (peers - 1), forward, 0)

    def settle(step, carry):
        frame = frame_at(step)
        keep(step, frame).wait()
        over_own(step, frame).wait_send()
        over(1 - aa, frame, 0).wait_recv()

        def each(i, c):
            send(step, frame, i).wait_send()
            over(aa, frame, i).wait_send()
            over(1 - aa, frame, i).wait_recv()
            return c

        lax.fori_loop(1, peers, each, 0)
        return carry

    lax.fori_loop(0, frames, settle, 0)

    @pl.when(ta < last)
    def _():
        for slot in range(LEFT):
            to_right(slot).wait_send()

    to_left.wait_send()


def exchange(voltages, window, signals, frames, peers):
    mat_hi, mat_lo = stage_two_matrix()
    dma = pltpu.SemaphoreType.DMA
    vmem = pl.BlockSpec(memory_space=pltpu.VMEM)
    hbm = pl.BlockSpec(memory_space=pltpu.HBM)
    mine = CH // peers
    return pl.pallas_call(
        functools.partial(exchange_kernel, signals, frames, peers),
        out_shape=jax.ShapeDtypeStruct((2, mine, frames * peers, 2, signals), jnp.bfloat16),
        in_specs=[hbm, vmem, vmem, vmem, vmem],
        out_specs=hbm,
        scratch_shapes=[
            pltpu.VMEM((LEFT + frames + 1, signals, NFFT), jnp.bfloat16),
            pltpu.VMEM((TAPS, NFFT), jnp.float32),
            pltpu.VMEM((HALF + 1, 2 * signals, 2 * INNER), jnp.bfloat16),
            pltpu.VMEM((2 * CH, signals), jnp.float32),
            pltpu.VMEM((frames, CH, 2, signals), jnp.bfloat16),
            dma((frames,)),
            dma((LEFT + 1,)),
            dma((LEFT + 1,)),
            dma((frames,)),
            dma((frames, peers)),
            dma((frames, peers)),
            dma((frames, peers)),
            dma((frames, peers)),
        ],
        compiler_params=pltpu.CompilerParams(
            collective_id=0, has_side_effects=True, vmem_limit_bytes=48 * 1024 * 1024
        ),
    )(voltages, window, jnp.asarray(twist_table()), jnp.asarray(mat_hi), jnp.asarray(mat_lo))


def correlate_kernel(block, signals, scale, place, grid_in, out):
    side = place[0]
    rows = grid_in.shape[2]
    dims = (((0,), (0,)), ((), ()))
    even = lax.broadcasted_iota(jnp.int32, (rows, signals), 0) % 2 == 0
    for c in range(block):
        left = grid_in[side, c]
        wide = left.astype(jnp.float32)
        turned = jnp.where(even, pltpu.roll(wide, rows - 1, 0), -pltpu.roll(wide, 1, 0))
        both = jnp.concatenate([left, turned.astype(jnp.bfloat16)], axis=1)
        against = jnp.concatenate([grid_in[0, c], grid_in[1, c]], axis=1)
        res = lax.dot_general(both, against, dims, preferred_element_type=jnp.float32) * scale
        out[c, :, : 2 * signals] = res[:signals]
        out[c, :, 2 * signals :] = res[signals:]


def correlate(spectra, place, scale):
    _, channels, rows, signals = spectra.shape
    block = 16 if rows <= 128 else 8
    return pl.pallas_call(
        functools.partial(correlate_kernel, block, signals, scale),
        grid_spec=pltpu.PrefetchScalarGridSpec(
            num_scalar_prefetch=1,
            grid=(channels // block,),
            in_specs=[pl.BlockSpec((2, block, rows, signals), lambda i, p: (0, i, 0, 0))],
            out_specs=pl.BlockSpec((block, signals, 4 * signals), lambda i, p: (i, 0, 0)),
        ),
        out_shape=jax.ShapeDtypeStruct((channels, signals, 4 * signals), jnp.float32),
        compiler_params=pltpu.CompilerParams(
            dimension_semantics=("arbitrary",), vmem_limit_bytes=40 * 1024 * 1024
        ),
    )(place.astype(jnp.int32).reshape(1), spectra)


def per_device(voltages, pfb_window):
    signals, samples = voltages.shape
    frames = samples // NFFT
    peers = lax.axis_size("ta")
    assert lax.axis_size("aa") == 2 and frames >= TAPS - 1 and signals == LANES
    spectra = exchange(voltages, pfb_window, signals, frames, peers)
    spectra = spectra.reshape(2, CH // peers, frames * peers * 2, signals)
    scale = 1.0 / math.sqrt(frames * peers)
    return correlate(spectra, lax.axis_index("aa"), scale)


def solution(mesh):
    return jax.shard_map(
        per_device, mesh=mesh, in_specs=(P("aa", "ta"), P()), out_specs=P("ta", "aa", None),
        check_vma=False,
    )
```

profile of v0, /device:TPU:10, one launch (start us, length us, event | category | flops | bytes accessed | tf_op | source)
XLA Modules:
  0.0 185.3 jit_solution(14295553583738637527)
XLA Ops:
  0.0 0.0 copy-start.1
  0.0 0.9 copy-done.1
  1.0 0.0 copy-start.2
  1.0 0.9 copy-done.2
  1.9 0.0 copy-start.3
  1.9 0.9 copy-done.3
  2.8 0.0 copy-start.4
  2.8 0.8 copy-done.4
  3.6 166.3 %shard_map.55 = bf16[2,128,48,2,128]{4,3,2,1,0:T(2,128)(2,1)} custom-call(bf16[128,24576]{1,0:T(8,128)(2,1)} %vol.1, f32[4,8192]{1,0:T(4,128)S(1)} %copy-done.3, f32[2,17,256]{2,1,0:T(8,128)S(1)} %copy-done.4, bf16[256,512]{1,0:T(8,128)(2,1)S(1)} %copy-done.2, bf16[256,512]{1,0:T(8,128)(2,1)S(1)} %copy-done.1), custom_call_target="tpu_custom_call" | custom-call | tf_op jit(solution)/shard_map/pallas_call | solution.py:308
  169.9 0.0 copy-start
  169.9 2.8 %copy-done = bf16[2,128,48,2,128]{4,3,2,1,0:T(2,128)(2,1)S(1)} copy-done((bf16[2,128,48,2,128]{4,3,2,1,0:T(2,128)(2,1)S(1)}, bf16[2,128,48,2,128]{4,3,2,1,0:T(2,128)(2,1)}, u32[]{:S(2)}) %copy-start) | copy-done | bytes 6291480
  172.7 12.6 %shard_map.56 = f32[128,128,512]{2,1,0:T(8,128)} custom-call(s32[1]{0:T(128)} %bitcast.place, bf16[2,128,96,128]{3,2,1,0:T(8,128)(2,1)S(1)} %bitcast.2), custom_call_target="tpu_custom_call" | custom-call | tf_op jit(solution)/shard_map/pallas_call | solution.py:353
Async XLA Ops:
  0.0 0.9 copy-start.1
  1.0 0.9 copy-start.2
  1.9 0.9 copy-start.3
  2.8 0.8 copy-start.4
  169.9 2.8 %copy-start = (bf16[2,128,48,2,128]{4,3,2,1,0:T(2,128)(2,1)S(1)}, bf16[2,128,48,2,128]{4,3,2,1,0:T(2,128)(2,1)}, u32[]{:S(2)}) copy-start(bf16[2,128,48,2,128]{4,3,2,1,0:T(2,128)(2,1)} %shard_map.55) | copy-start | bytes 18874372
where the time goes:
time: 186 us; the launch traced here: 185 us
  Pallas kernels  179 us (96%)
  local copies, waits for them, and re-layouts  6.38 us (3%)
    pallas_call x1, Pallas kernels, exchange(): pl.pallas_call(functools.partial(exchange_kernel, signals, frames, peers)...  166 us
    pallas_call x1, Pallas kernels, correlate(): pl.pallas_call(functools.partial(correlate_kernel, block, signals, scale)...  12.6 us
    unnamed x10, local copies, waits for them, and re-layouts  6.38 us

commit v1 on v0

v1 whole, which is shorter than its diff:
```python
import functools
import math

import jax
import jax.numpy as jnp
import numpy as np
from jax import lax
from jax.experimental import pallas as pl
from jax.experimental.pallas import tpu as pltpu
from jax.sharding import PartitionSpec as P

NFFT = 8192
CH = 2048
TAPS = 4
CH_OFF = 1024
RADIX = 32
INNER = NFFT // RADIX
BINS = CH // RADIX
HALF = RADIX // 2
LANES = 128
SIG_BLOCK = 16
MESH = pl.DeviceIdType.MESH


def split_bf16(x):
    hi = jnp.asarray(x, jnp.bfloat16)
    return hi, (x - hi.astype(jnp.float32)).astype(jnp.bfloat16)


def stage_two_matrix():
    n2 = np.arange(INNER)[None, :]
    m = np.arange(BINS)[:, None] + CH_OFF // RADIX
    angle = 2.0 * np.pi * ((n2 * m) % INNER) / INNER
    mirror = 2.0 * np.pi * ((n2 * (m + 1)) % INNER) / INNER
    rows = [
        np.concatenate([np.cos(angle), np.sin(angle)], axis=1),
        np.concatenate([-np.sin(angle), np.cos(angle)], axis=1),
        np.concatenate([np.cos(mirror), -np.sin(mirror)], axis=1),
        np.concatenate([-np.sin(mirror), -np.cos(mirror)], axis=1),
    ]
    full = np.concatenate(rows, axis=0) / math.sqrt(NFFT)
    hi = full.astype(jnp.bfloat16)
    lo = (full - hi.astype(np.float64)).astype(jnp.bfloat16)
    return hi, lo


def twist_table():
    k = np.arange(HALF + 1)[:, None]
    n2 = np.arange(INNER)[None, :]
    angle = 2.0 * np.pi * (k * n2) / NFFT
    return np.stack([np.cos(angle), -np.sin(angle)]).astype(np.float32)


def rfft_list(x):
    n = len(x)
    if n == 2:
        return [(x[0] + x[1], None), (x[0] - x[1], None)]
    even, odd = rfft_list(x[0::2]), rfft_list(x[1::2])
    out = [None] * (n // 2 + 1)
    for k in range(n // 4 + 1):
        er, ei = even[k]
        our, oui = odd[k]
        if k == 0:
            out[0] = (er + our, None)
            out[n // 2] = (er - our, None)
        elif k == n // 4:
            out[k] = (er, -our)
        else:
            c = math.cos(2 * math.pi * k / n)
            s = math.sin(2 * math.pi * k / n)
            if 8 * k == n:
                tr, ti = (our + oui) * c, (oui - our) * c
            else:
                tr, ti = our * c + oui * s, oui * c - our * s
            out[k] = (er + tr, ei + ti)
            out[n // 2 - k] = (er - tr, ti - ei)
    return out


def pair(a, b, peers):
    total, bit = 0, 1
    while bit < peers:
        total = total + (a // bit + b // bit) % 2 * bit
        bit *= 2
    return total


def channel_frame(signals, volts, win, twist, mat_hi, mat_lo, parts_s, spec):
    taps = volts.shape[0]

    def block(step, carry):
        rows = pl.ds(pl.multiple_of(step * SIG_BLOCK, SIG_BLOCK), SIG_BLOCK)
        low_rows = pl.ds(pl.multiple_of(signals + step * SIG_BLOCK, SIG_BLOCK), SIG_BLOCK)
        for part in range(INNER // LANES):
            filtered = []
            for n1 in range(RADIX):
                cols = pl.ds(n1 * INNER + part * LANES, LANES)
                total = win[0:1, cols] * volts[0, rows, cols].astype(jnp.float32)
                for t in range(1, taps):
                    total = total + win[t : t + 1, cols] * volts[t, rows, cols].astype(jnp.float32)
                filtered.append(total)
            here = pl.ds(part * LANES, LANES)
            there = pl.ds(INNER + part * LANES, LANES)
            for k, (ar, ai) in enumerate(rfft_list(filtered)):
                if k == 0:
                    br, bi = ar, jnp.zeros_like(ar)
                else:
                    tr, ti = twist[0, k : k + 1, here], twist[1, k : k + 1, here]
                    if ai is None:
                        br, bi = ar * tr, ar * ti
                    else:
                        br, bi = ar * tr - ai * ti, ar * ti + ai * tr
                for value, cols in ((br, here), (bi, there)):
                    hi, lo = split_bf16(value)
                    parts_s[k, rows, cols] = hi
                    parts_s[k, low_rows, cols] = lo
        return carry

    lax.fori_loop(0, signals // SIG_BLOCK, block, 0)
    dims = (((1,), (1,)), ((), ()))

    def dot(a, b):
        return lax.dot_general(a, b, dims, preferred_element_type=jnp.float32)

    def put(value, k):
        spec[pl.ds(2 * k, BINS, stride=2 * RADIX), :] = value[:BINS]
        spec[pl.ds(2 * k + 1, BINS, stride=2 * RADIX), :] = value[BINS:]

    for k in range(HALF + 1):
        size = 2 * BINS if k in (0, HALF) else 4 * BINS
        a_hi, a_lo = mat_hi[:size, :], mat_lo[:size, :]
        both = dot(a_hi, parts_s[k])
        small = dot(a_lo, parts_s[k, :signals])
        res = both[:, :signals] + (both[:, signals:] + small)
        put(res[: 2 * BINS], k)
        if size > 2 * BINS:
            put(res[2 * BINS :], RADIX - k)


def exchange_kernel(signals, frames, peers, vol, win_in, twist_in, hi_in, lo_in, grid_out,
                    volts, win, twist, mat_hi, mat_lo, weff, parts_s, spec, give, take, take_wide, done,
                    const_sem, load_sem, give_send, give_recv, own_sem, send_sem, recv_sem, over_send, over_recv):
    ta, aa = lax.axis_index("ta"), lax.axis_index("aa")
    core, side = ta % 2, ta // 2 % 2
    last = peers - 1
    mine = CH // peers
    wide = 2 * mine
    half = peers // 2
    right, left = (ta + 1) % peers, (ta + last) % peers
    near = ta + 1 - 2 * core
    far = jnp.where(core == 0, left, right)

    copy = pltpu.make_async_copy
    consts = [
        copy(source, target, const_sem.at[slot])
        for slot, (source, target) in enumerate(
            ((win_in, win), (twist_in, twist), (hi_in, mat_hi), (lo_in, mat_lo)))
    ]
    loads = [
        copy(vol.at[:, pl.ds(f * NFFT, NFFT)], volts.at[f], load_sem.at[f]) for f in range(frames)
    ]
    for one in consts + loads:
        one.start()

    barrier = pltpu.get_barrier_semaphore()

    def greet(i, carry):
        pl.semaphore_signal(barrier, 1, device_id=(pair(ta, i, peers), aa), device_id_type=MESH)
        return carry

    lax.fori_loop(1, peers, greet, 0)
    pl.semaphore_signal(barrier, 1, device_id=(ta, 1 - aa), device_id_type=MESH)
    for one in consts + loads:
        one.wait()
    pl.semaphore_wait(barrier, peers)

    def edge(kind):
        return jnp.where(core == kind, ta, right)

    def owner(kind, j):
        return jnp.where(kind == 0, j // 2 * 4 + 2 * side + j % 2, 2 * j + core)

    def give_far(f):
        return pltpu.make_async_remote_copy(
            give.at[f], take.at[f], give_send.at[f], give_recv.at[f],
            device_id=(far, aa), device_id_type=MESH)

    def give_near(f):
        return pltpu.make_async_remote_copy(
            spec.at[frames + f].reshape(half, 2, wide, signals).at[:, 1 - core], take_wide.at[f],
            give_send.at[frames + f], give_recv.at[frames + f],
            device_id=(near, aa), device_id_type=MESH)

    def place(which, boundary, f):
        return grid_out.at[which, :, boundary * frames + f]

    def block(kind, f, j):
        return done.at[kind * frames + f, pl.ds(j * mine, mine)]

    def send(kind, f, j):
        return pltpu.make_async_remote_copy(
            block(kind, f, j), place(aa, edge(kind), f),
            send_sem.at[kind * frames + f, j], recv_sem.at[edge(kind), f],
            device_id=(owner(kind, j), aa), device_id_type=MESH)

    def own_block(kind):
        return jnp.where(kind == 0, ta // 4 * 2 + core, ta // 2)

    def keep(kind, f):
        return copy(block(kind, f, own_block(kind)), place(aa, edge(kind), f), own_sem.at[kind * frames + f])

    def over_own(kind, f):
        return pltpu.make_async_remote_copy(
            block(kind, f, own_block(kind)), place(aa, edge(kind), f),
            over_send.at[edge(kind), f], over_recv.at[edge(kind), f],
            device_id=(ta, 1 - aa), device_id_type=MESH)

    def maker(boundary):
        before = (boundary + last) % peers
        by_core = before + core
        by_side = jnp.where(boundary // 2 % 2 == side, boundary, before)
        return jnp.where(boundary % 2 == 1, by_core, by_side)

    def arrival(boundary, f):
        here = place(aa, boundary, f)
        return pltpu.make_async_remote_copy(
            here, here, send_sem.at[0, 0], recv_sem.at[boundary, f],
            device_id=(maker(boundary), aa), device_id_type=MESH)

    def over(which, boundary, f):
        here = place(which, boundary, f)
        return pltpu.make_async_remote_copy(
            here, here, over_send.at[boundary, f], over_recv.at[boundary, f],
            device_id=(ta, 1 - aa), device_id_type=MESH)

    def transform(kind, f):
        before = core == kind
        for j in range(frames):
            tap = jnp.where(before, j + TAPS - 1 - f, j - f)
            used = (tap >= 0) & (tap < TAPS) & (before & (tap >= TAPS - 1 - f) | ~before & (tap < TAPS - 1))
            used = used & (before | (ta < last))
            row = pl.ds(jnp.clip(tap, 0, TAPS - 1), 1)
            weff[j : j + 1, :] = win[row, :] * jnp.where(used, 1.0, 0.0).astype(jnp.float32)
        channel_frame(signals, volts, weff, twist, mat_hi, mat_lo, parts_s, spec.at[kind * frames + f])

    def far_first(f, carry):
        transform(0, f)

        def pack(j, c):
            rows = pl.ds(pl.multiple_of((j // 2 * 4 + 2 * (1 - side) + j % 2) * wide, wide), wide)
            give[f, pl.ds(pl.multiple_of(j * wide, wide), wide), :] = spec[f, rows, :].astype(jnp.bfloat16)
            return c

        lax.fori_loop(0, half, pack, 0)
        give_far(f).start()
        return carry

    def finish(kind, f):
        def add(j, c):
            here = pl.ds(pl.multiple_of(j * wide, wide), wide)
            rows = pl.ds(pl.multiple_of(owner(kind, j) * wide, wide), wide)
            if kind == 0:
                other = take[f, here, :].astype(jnp.float32)
            else:
                other = take_wide[f, j]
            total = spec[kind * frames + f, rows, :] + other
            done.at[kind * frames + f].reshape(CH, signals)[here, :] = total.astype(jnp.bfloat16)
            return c

        lax.fori_loop(0, half, add, 0)
        over_own(kind, f).start()
        keep(kind, f).start()

        def each(n, c):
            j = pair(own_block(kind), half - 1 - n, half)
            send(kind, f, j).start()
            return c

        lax.fori_loop(0, half - 1, each, 0)

    def finish_far(f):
        give_far(f).wait_recv()
        finish(0, f)

    def forward(kind, f):
        def each(q, c):
            boundary = 2 * pair(ta // 2, q, half) + kind

            @pl.when(maker(boundary) != ta)
            def _():
                arrival(boundary, f).wait_recv()
                over(aa, boundary, f).start()

            return c

        lax.fori_loop(0, half, each, 0)

    def near_step(f, carry):
        transform(1, f)
        give_near(f).start()
        finish_far(f)
        give_near(f).wait_recv()
        finish(1, f)
        @pl.when(f > 0)
        def _():
            forward(0, f - 1)
            forward(1, f - 1)

        return carry

    lax.fori_loop(0, frames, far_first, 0)
    lax.fori_loop(0, frames, near_step, 0)
    forward(0, frames - 1)
    forward(1, frames - 1)

    def settle(f, carry):
        give_far(f).wait_send()
        give_near(f).wait_send()
        for kind in range(2):
            keep(kind, f).wait()

            def each(n, c):
                send(kind, f, pair(own_block(kind), half - 1 - n, half)).wait_send()
                return c

            lax.fori_loop(0, half - 1, each, 0)

        def crossed(boundary, c):
            over(aa, boundary, f).wait_send()
            over(1 - aa, boundary, f).wait_recv()
            return c

        lax.fori_loop(0, peers, crossed, 0)
        return carry

    lax.fori_loop(0, frames, settle, 0)


def exchange(voltages, window, signals, frames, peers):
    mat_hi, mat_lo = stage_two_matrix()
    dma = pltpu.SemaphoreType.DMA
    hbm = pl.BlockSpec(memory_space=pltpu.HBM)
    mine = CH // peers
    return pl.pallas_call(
        functools.partial(exchange_kernel, signals, frames, peers),
        out_shape=jax.ShapeDtypeStruct((2, mine, frames * peers, 2, signals), jnp.bfloat16),
        in_specs=[hbm] * 5,
        out_specs=hbm,
        scratch_shapes=[
            pltpu.VMEM((frames, signals, NFFT), jnp.bfloat16),
            pltpu.VMEM((TAPS, NFFT), jnp.float32),
            pltpu.VMEM((2, HALF + 1, INNER), jnp.float32),
            pltpu.VMEM((4 * BINS, 2 * INNER), jnp.bfloat16),
            pltpu.VMEM((4 * BINS, 2 * INNER), jnp.bfloat16),
            pltpu.VMEM((frames, NFFT), jnp.float32),
            pltpu.VMEM((HALF + 1, 2 * signals, 2 * INNER), jnp.bfloat16),
            pltpu.VMEM((2 * frames, 2 * CH, signals), jnp.float32),
            pltpu.VMEM((frames, CH, signals), jnp.bfloat16),
            pltpu.VMEM((frames, CH, signals), jnp.bfloat16),
            pltpu.VMEM((frames, peers // 2, 2 * mine, signals), jnp.float32),
            pltpu.VMEM((2 * frames, CH // 2, 2, signals), jnp.bfloat16),
            dma((4,)),
            dma((frames,)),
            dma((2 * frames,)),
            dma((2 * frames,)),
            dma((2 * frames,)),
            dma((2 * frames, peers // 2)),
            dma((peers, frames)),
            dma((peers, frames)),
            dma((peers, frames)),
        ],
        compiler_params=pltpu.CompilerParams(
            collective_id=0, has_side_effects=True, vmem_limit_bytes=62 * 1024 * 1024
        ),
    )(voltages, window, jnp.asarray(twist_table()), jnp.asarray(mat_hi), jnp.asarray(mat_lo))


def correlate_kernel(block, signals, scale, place, grid_in, out):
    side = place[0]
    rows = grid_in.shape[2]
    dims = (((0,), (0,)), ((), ()))
    even = lax.broadcasted_iota(jnp.int32, (rows, signals), 0) % 2 == 0
    for c in range(block):
        left = grid_in[side, c]
        wide = left.astype(jnp.float32)
        turned = jnp.where(even, pltpu.roll(wide, rows - 1, 0), -pltpu.roll(wide, 1, 0))
        both = jnp.concatenate([left, turned.astype(jnp.bfloat16)], axis=1)
        against = jnp.concatenate([grid_in[0, c], grid_in[1, c]], axis=1)
        res = lax.dot_general(both, against, dims, preferred_element_type=jnp.float32) * scale
        out[c, :, : 2 * signals] = res[:signals]
        out[c, :, 2 * signals :] = res[signals:]


def correlate(spectra, place, scale):
    _, channels, rows, signals = spectra.shape
    block = 16 if rows <= 128 else 8
    return pl.pallas_call(
        functools.partial(correlate_kernel, block, signals, scale),
        grid_spec=pltpu.PrefetchScalarGridSpec(
            num_scalar_prefetch=1,
            grid=(channels // block,),
            in_specs=[pl.BlockSpec((2, block, rows, signals), lambda i, p: (0, i, 0, 0))],
            out_specs=pl.BlockSpec((block, signals, 4 * signals), lambda i, p: (i, 0, 0)),
        ),
        out_shape=jax.ShapeDtypeStruct((channels, signals, 4 * signals), jnp.float32),
        compiler_params=pltpu.CompilerParams(
            dimension_semantics=("arbitrary",), vmem_limit_bytes=62 * 1024 * 1024
        ),
    )(place.astype(jnp.int32).reshape(1), spectra)


def per_device(voltages, pfb_window):
    signals, samples = voltages.shape
    frames = samples // NFFT
    peers = lax.axis_size("ta")
    assert lax.axis_size("aa") == 2 and frames == TAPS - 1 and signals == LANES
    spectra = exchange(voltages, pfb_window, signals, frames, peers)
    spectra = spectra.reshape(2, CH // peers, frames * peers * 2, signals)
    scale = 1.0 / math.sqrt(frames * peers)
    return correlate(spectra, lax.axis_index("aa"), scale)


def solution(mesh):
    return jax.shard_map(
        per_device, mesh=mesh, in_specs=(P("aa", "ta"), P()), out_specs=P("ta", "aa", None),
        check_vma=False,
    )
```

time: 186 us -> 139 us (0.75)
  the two profiles are of different devices: /device:TPU:10 before, /device:TPU:0 now
where the time goes in v1:
time: 139 us
  Pallas kernels  139 us (100%)
    pallas_call x1, Pallas kernels, exchange(): pl.pallas_call(functools.partial(exchange_kernel, signals, frames, peers)...  125 us
    pallas_call x1, Pallas kernels, correlate(): pl.pallas_call(functools.partial(correlate_kernel, block, signals, scale)...  14.3 us

profile of v1, /device:TPU:0, one launch (start us, length us, event | category | flops | bytes accessed | tf_op | source)
XLA Modules:
  0.0 139.0 jit_solution(6619540082377433778)
XLA Ops:
  0.0 124.7 %shard_map.55 = bf16[2,128,48,2,128]{4,3,2,1,0:T(2,128)(2,1)} custom-call(bf16[128,24576]{1,0:T(8,128)(2,1)} %vol.1, f32[4,8192]{1,0:T(4,128)} %win_in.1, f32[2,17,256]{2,1,0:T(8,128)} %constant.10.clone.twist_in, bf16[256,512]{1,0:T(8,128)(2,1)} %constant.11.clone.hi_in, bf16[256,512]{1,0:T(8,128)(2,1)} %constant.12.clone.lo_in), custom_call_target="tpu_custom_call" | custom-call | tf_op jit(solution)/shard_map/pallas_call | solution.py:344
  124.8 14.3 %shard_map.56 = f32[128,128,512]{2,1,0:T(8,128)} custom-call(s32[1]{0:T(128)} %bitcast.place, bf16[2,128,96,128]{3,2,1,0:T(8,128)(2,1)} %bitcast.2), custom_call_target="tpu_custom_call" | custom-call | tf_op jit(solution)/shard_map/pallas_call | solution.py:397
